TPU v7x, 32 devices: a whole 2x2x4 slice. The times are simulated.
32 devices in a mesh: parts: 2 (over x), rows: 16 (over z, y, core).
Axes of the slice: x: 2, y: 2, z: 4, core: 2. Of those that a mesh axis runs over, the one named last changes fastest.
Arguments:
- feature_bin: int32 [16384, 700], P(('parts', 'rows')), parts along dimension 0, may hold values from 0 to 255
- doc_leaf: int32 [16384], P(('parts', 'rows')), parts along dimension 0, may hold values from 0 to 31
- current_score: float32 [16384], P(('parts', 'rows')), parts along dimension 0, may hold values from -8 to 8
- relevance: int32 [16384], P(('parts', 'rows')), parts along dimension 0, may hold values from 0 to 4
- doc_rank: int32 [16384], P(('parts', 'rows')), parts along dimension 0, may hold values from 0 to 255, as said below
- query_length: int32 [64], P(('parts', 'rows')), parts along dimension 0, may hold values from 10 to 256, as said below
- feature_votes: int32 [32, 32, 20], P(('parts', 'rows')), parts along dimension 0, may hold values from 0 to 699, all different within a row
- elected: int32 [64, 40], P('parts'), parts along dimension 0, may hold values from 0 to 699, all different within a row
Outputs:
- gradient: float32 [16384], P(('parts', 'rows')), parts along dimension 0
- hessian: float32 [16384], P(('parts', 'rows')), parts along dimension 0
- vote_count: int32 [64, 700], P('parts'), parts along dimension 0
- split_gain: float32 [64, 40, 256], P('parts'), parts along dimension 0
There are 2 independent parts, one for each index of `parts`. A program takes and returns all parts, laid end to end along the dimension named above; each array names one. Nothing has to cross between parts.
Inputs may be any that keep to these rules, and one draw needn't show every extreme that they name: `query_length`: query q holds slots q * 256 to (q + 1) * 256 - 1 of the document arrays; in every draw some query has exactly 256 documents. `doc_rank`: within each query the live documents hold positions 0 to query_length - 1, each once; slots that are not live hold positions from query_length to 255. `feature_votes`: the 20 votes of one device for one leaf are different features. The 40 elected features of one leaf are different.
All inputs are finite; a program needn't handle non-finite values.
Results may differ from a plain program's by a relative error of at most 0.0003.
Values sent between devices are 32-bit elements; how exact they have to be, the bound alone decides.
A program may use at most 64 MiB of HBM per device.

v0:
```python
import math

import jax
import jax.numpy as jnp
from jax import lax
from jax.sharding import PartitionSpec as P

B = 256
QMAX = 256


ridge_weight = 1.0


def query_terms(scores, levels, places, length):
    positions = jnp.arange(scores.shape[0], dtype=jnp.int32)
    living = positions < length
    gains = jnp.exp2(levels.astype(jnp.float32)) - 1.0
    discount = 1.0 / jnp.log2(places.astype(jnp.float32) + 2.0)
    higher = (levels[None, :] > levels[:, None]) & living[None, :]
    earlier = (
        (levels[None, :] == levels[:, None])
        & (positions[None, :] < positions[:, None])
        & living[None, :]
    )
    ideal_place = jnp.sum((higher | earlier).astype(jnp.float32), axis=1)
    ideal = jnp.sum(jnp.where(living, gains / jnp.log2(ideal_place + 2.0), 0.0))
    scaling = 1.0 / jnp.maximum(ideal, 1.0)
    ordered = (levels[:, None] > levels[None, :]) & living[:, None] & living[None, :]
    chance = jax.nn.sigmoid(scores[None, :] - scores[:, None])
    change = (
        (gains[:, None] - gains[None, :]) * jnp.abs(discount[:, None] - discount[None, :]) * scaling
    )
    pushes = jnp.where(ordered, chance * change, 0.0)
    curves = jnp.where(ordered, chance * (1.0 - chance) * change, 0.0)
    return (
        jnp.sum(pushes, axis=0) - jnp.sum(pushes, axis=1),
        jnp.sum(curves, axis=0) + jnp.sum(curves, axis=1),
    )


def build_histogram(feature_bin, doc_leaf, gradient, hessian, elected, bins):
    leaves, picked = elected.shape
    documents = feature_bin.shape[0]
    leaf_hot = (doc_leaf[:, None] == jnp.arange(leaves, dtype=jnp.int32)[None, :]).astype(
        jnp.float32
    )
    columns = jnp.dot(
        leaf_hot, elected.astype(jnp.float32), precision=lax.Precision.HIGHEST
    ).astype(jnp.int32)
    chosen = jnp.take_along_axis(feature_bin, columns, axis=1)
    weighted = jnp.concatenate([leaf_hot * gradient[:, None], leaf_hot * hessian[:, None]], axis=1)
    block_rows = math.gcd(documents, 512)
    block_count = documents // block_rows
    bin_ids = jnp.arange(bins, dtype=jnp.int32)

    def add_block(index, total):
        onehot = (chosen[:, :, None] == bin_ids[None, None, :]).astype(jnp.float32)
        onehot = onehot.reshape(block_rows, picked * bins)
        return total + jnp.dot(weighted.T, onehot, precision=lax.Precision.HIGHEST)

    empty = jnp.zeros((2 * leaves, picked * bins), jnp.float32)
    total = lax.fori_loop(0, block_count, add_block, empty)
    return total.reshape(2, leaves, picked, bins)


def split_score(prefix, whole):
    remain = whole - prefix
    return (
        prefix[0] * prefix[0] / (prefix[1] + ridge_weight)
        + remain[0] * remain[0] / (remain[1] + ridge_weight)
        - whole[0] * whole[0] / (whole[1] + ridge_weight)
    )


def count_votes(feature_votes, features):
    hits = feature_votes[..., None] == jnp.arange(features, dtype=jnp.int32)
    return jnp.sum(hits.astype(jnp.int32), axis=(0, 2))


def on_device(
    feature_bin, doc_leaf, current_score, relevance, doc_rank, query_length, feature_votes, elected
):
    features = feature_bin.shape[1]
    all_votes = lax.all_gather(feature_votes, "rows", axis=0, tiled=True)
    vote_count = count_votes(all_votes, features)

    def one_query(items):
        return query_terms(items[0], items[1], items[2], items[3])

    gradient, hessian = lax.map(
        one_query,
        (
            current_score.reshape(-1, QMAX),
            relevance.reshape(-1, QMAX),
            doc_rank.reshape(-1, QMAX),
            query_length,
        ),
    )
    gradient = gradient.reshape(-1)
    hessian = hessian.reshape(-1)
    histogram = build_histogram(feature_bin, doc_leaf, gradient, hessian, elected, B)
    summed = lax.psum(histogram, "rows")
    prefix = jnp.cumsum(summed, axis=3)
    whole = jnp.sum(summed, axis=3, keepdims=True)
    split_gain = split_score(prefix, whole)
    return (gradient, hessian, vote_count, split_gain)


def solution(mesh):
    return jax.shard_map(
        on_device,
        mesh=mesh,
        in_specs=(
            P(("parts", "rows"), None),
            P(("parts", "rows")),
            P(("parts", "rows")),
            P(("parts", "rows")),
            P(("parts", "rows")),
            P(("parts", "rows")),
            P(("parts", "rows"), None, None),
            P("parts", None),
        ),
        out_specs=(
            P(("parts", "rows")),
            P(("parts", "rows")),
            P("parts", None),
            P("parts", None, None),
        ),
        check_vma=False,
    )
```

profile of v0, /device:TPU:0, one launch (start us, length us, event | category | flops | bytes accessed | tf_op | source)
XLA Modules:
  0.0 409.0 jit_solution(16073954382203800596)
XLA Ops:
  7.3 0.8 reshape.169
  8.0 0.7 reshape.170
  8.7 0.7 reshape.171
  9.4 9.2 %while.18 = (s32[]{:T(128)}, f32[2,256]{1,0:T(2,128)S(1)}, f32[2,256]{1,0:T(2,128)S(1)}, s32[2,256]{1,0:T(2,128)S(1)}, s32[2]{0:T(128)}, /*index=5*/f32[2,256]{1...) while((s32[]{:T(128)}, f32[2,256]{1,0:T(2,128)S(1)}, f32[2,256]{1,0:T(2,128)S(1)}, ...), condition=%wide.region_7.8_spmd, body=%wide.region_0.7_spmd.sunk | while | flops 2035203 | bytes 32681 | solution.py:91
  9.5 1.2 dynamic_slice.34
  10.7 0.6 iota_compare_fusion.6
  11.4 0.2 convert_reduce_fusion.3
  11.6 1.3 exponential_add_fusion.5
  13.5 0.4 fusion.28
  14.1 1.2 dynamic_slice.34
  15.3 0.6 iota_compare_fusion.6
  16.2 1.3 exponential_add_fusion.5
  18.2 0.4 fusion.28
  18.7 1.0 bitcast_or_fusion
  20.0 163.1 %gather_fusion = s32[20480]{0:T(1024)S(1)} fusion(s32[512,700]{0,1:T(8,128)S(1)} %copy-done, s32[20480]{0:T(1024)S(1)} %reshape.179), kind=kCustom, calls=%fused_computation | custom fusion | bytes 327680 | tf_op jit(solution)/shard_map/jit(take_along_axis)/gather | solution.py:51
  183.5 3.3 bitcast_compare_fusion
  186.8 11.0 %fusion.22 = f32[2,32,40,256]{3,1,2,0:T(8,128)} fusion(f32[2,32,512,1]{2,1,3,0:T(8,128)S(1)} %bitcast.69, pred[40,256,512,1]{2,1,0,3:T(32,128)(4,1)S(1)} %bitcast.68), kind=kOutput, calls=%fused_computation.56 | convolution fusion | flops 4026531840 | bytes 7995392 | tf_op jit(solution)/shard_map/while/body/eval_jaxpr/dot_general | solution.py:60
  197.9 0.7 copy-done.2
  198.6 24.5 %all_gather.3 = s32[16,32,20]{1,2,0:T(8,128)S(1)} all-gather(s32[1,32,20]{1,2,0:T(8,128)S(1)} %copy.33), channel_id=1, replica_groups=mesh['parts'=2,'rows'=16] {'rows'}, dimensions={0}, use_global_device_ids=true | all-gather | bytes 43520 | tf_op jit(solution)/shard_map/all_gather | solution.py:85
  223.1 4.4 %convert_reduce_fusion.1 = s32[32,700]{1,0:T(8,128)} fusion(s32[16,32,20]{1,2,0:T(8,128)S(1)} %all_gather.3), kind=kLoop, calls=%fused_computation.25 | loop fusion | flops 21481600 | bytes 130560 | tf_op jit(solution)/shard_map/reduce_sum | solution.py:78
  227.5 74.4 %all-reduce.2.cloned.1.call-done = f32[2,32,40,256]{3,1,2,0:T(8,128)} async-done(((f32[2,32,40,256]{3,1,2,0:T(8,128)}), f32[2,32,40,256]{3,1,2,0:T(8,128)}) %all-reduce.2.cloned.1.call-update) | async-done | bytes 2621456 | tf_op jit(solution)/shard_map/psum | solution.py:103
  302.0 2.2 reduce_sum.91
  304.2 4.3 %reshape.175 = f32[2,32,40,2,128]{4,3,1,2,0:T(2,128)} reshape(f32[2,32,40,256]{3,1,2,0:T(8,128)} %all-reduce.2.cloned.1.call-done) | data formatting | bytes 5242880 | tf_op jit(solution)/shard_map/reshape.2
  308.5 4.8 %copy.36 = f32[2,32,40,2,128]{4,2,3,1,0:T(8,128)} copy(f32[2,32,40,2,128]{4,3,1,2,0:T(2,128)} %reshape.175) | data formatting | bytes 5242880 | tf_op jit(solution)/shard_map/reshape.2
  313.3 69.9 %reduce-window.6 = f32[2,32,40,2,128]{4,2,3,1,0:T(8,128)} reduce-window(f32[2,32,40,2,128]{4,2,3,1,0:T(8,128)} %copy.36, f32[]{:T(128)} %constant.79.clone.1), window={size=1x1x1x1x128 pad=0_0x0_0x0_0x0_0x127_0}, to_apply=%region_10.11 | reduce-window | flops 83230720 | bytes 5242884 | tf_op jit(solution)/shard_map/reduce-window
  383.1 4.0 slice.41
  387.1 2.7 copy.37
  390.0 2.3 broadcast_add_fusion
  392.5 2.3 bitcast_subtract_fusion
  395.0 1.7 copy.39
  396.7 2.3 div.58
  399.1 3.1 fusion.12
  (47 shorter events, 1.9 us)
Async XLA Ops:
  7.2 12.8 %copy-start = (s32[512,700]{0,1:T(8,128)S(1)}, s32[512,700]{0,1:T(8,128)}, u32[]{:S(2)}) copy-start(s32[512,700]{0,1:T(8,128)} %param.10) | copy-start | bytes 4300804
  7.2 294.8 %all-reduce.2.cloned.1.call-start = ((), (), s32[]{:S(2)}) async-start(), calls=%async_computation | async-start | bytes 5242880 | tf_op jit(solution)/shard_map/psum | solution.py:103
  18.6 164.8 %copy-start.3 = (f32[1,2,2,128]{3,1,2,0:T(2,128)}, f32[1,2,2,128]{3,1,2,0:T(2,128)S(1)}, u32[]{:S(2)}) copy-start(f32[1,2,2,128]{3,1,2,0:T(2,128)S(1)} %copy.45) | copy-start | bytes 6148
  18.7 164.8 %copy-start.4 = (f32[1,2,2,128]{3,1,2,0:T(2,128)}, f32[1,2,2,128]{3,1,2,0:T(2,128)S(1)}, u32[]{:S(2)}) copy-start(f32[1,2,2,128]{3,1,2,0:T(2,128)S(1)} %copy.46) | copy-start | bytes 6148
  20.0 163.4 %copy-start.5 = (s32[512]{0:T(512)S(1)}, s32[512]{0:T(512)}, u32[]{:S(2)}) copy-start(s32[512]{0:T(512)} %param.11) | copy-start | bytes 6148
  197.9 0.7 copy-start.2
  390.0 2.5 copy-start.1
Sparse Core Ops, SparseCore 0:
  198.0 103.8 all-reduce.1
where the time goes:
time: 417 us; the launch traced here: 409 us
  local copies, waits for them, and re-layouts  189 us (45%)
  other arithmetic  92.9 us (22%)
  waiting for transfers between devices  74.4 us (18%)
  blocking collectives  24.5 us (6%)
  between operations  14.3 us (3%)
  matrix products  12 us (3%)
    gather x5, local copies, waits for them, and re-layouts, build_histogram(): chosen = jnp.take_along_axis(feature_bin, columns, axis=1)  164 us
    psum x1, waiting for transfers between devices, on_device(): summed = lax.psum(histogram, 'rows')  74.4 us
    another operation x5, other arithmetic  72.3 us
    all_gather x1, blocking collectives, on_device(): all_votes = lax.all_gather(feature_votes, 'rows', axis=0, tiled=True)  24.5 us
    dot_general x1, matrix products, add_block(): return total + jnp.dot(weighted.T, onehot, precision=lax.Precision.HIGHEST)  11 us
    another operation x4, local copies, waits for them, and re-layouts  9.1 us
  transfers between devices with their start and end apart: 1, of which 1 were waited for; matrix products, arithmetic and copies ran while one was open for 1% of the time, Pallas kernels for 0%

commit v1 on v0

v1 whole, which is shorter than its diff:
```python
import functools
import math

import jax
import jax.numpy as jnp
from jax import lax
from jax.experimental import pallas as pl
from jax.experimental.pallas import tpu as pltpu
from jax.sharding import PartitionSpec as P

B = 256
QMAX = 256
LANES = 128
TERMS = 3

ridge_weight = 1.0
F32 = jnp.float32
BF16 = jnp.bfloat16
NT = (((1,), (1,)), ((), ()))
VMEM = pl.BlockSpec(memory_space=pltpu.VMEM)


def slot_of(owner, turn, n):
    return turn * n + (owner % 2) * (n // 2) + owner // 2


def local_kernel(n, turns, fb_ref, leaf_ref, score_ref, rel_ref, rank_ref, qlen_ref, elected_ref,
                 votes_ref, send_ref, grad_ref, hess_ref, packed_ref, hot_ref, stack_ref, all_ref):
    docs, features = fb_ref.shape
    leaves, picked = elected_ref.shape
    chunks = docs // LANES
    per_query = QMAX // LANES

    groups = leaves // 8
    pitch = LANES // groups
    packed_ref[...] = jnp.full(packed_ref.shape, -1, jnp.int32)
    for g in range(groups):
        packed_ref[:, g * pitch:g * pitch + votes_ref.shape[2]] = votes_ref[0, g * 8:(g + 1) * 8, :]

    lanes = lax.broadcasted_iota(jnp.int32, (leaves, features), 1)
    for e in range(picked):
        hot_ref[e * leaves:(e + 1) * leaves, :] = jnp.where(
            elected_ref[:, e:e + 1] == lanes, 1.0, 0.0).astype(BF16)
    bins = fb_ref[...].astype(F32).astype(BF16)
    all_ref[...] = lax.dot_general(hot_ref[...], bins, NT, preferred_element_type=F32)

    rel = rel_ref[...].astype(F32)
    gain = jnp.exp2(rel) - 1.0
    disc = math.log(2.0) / jnp.log(rank_ref[...].astype(F32) + 2.0)
    row = lax.broadcasted_iota(jnp.int32, (chunks, LANES), 0)
    slot = (row % per_query) * LANES + lax.broadcasted_iota(jnp.int32, (chunks, LANES), 1)
    length = jnp.zeros((chunks, LANES), jnp.int32)
    for q in range(chunks // per_query):
        length = jnp.where(row // per_query == q, qlen_ref[q], length)
    live = slot < length
    livef = jnp.where(live, 1.0, 0.0)
    key = rel * float(QMAX) + (QMAX - 1 - slot).astype(F32)
    score = score_ref[...]
    stack_ref[...] = jnp.zeros(stack_ref.shape, F32)
    for index, item in enumerate((score, gain, disc, jnp.where(live, key, -1.0), livef)):
        stack_ref[index * chunks:(index + 1) * chunks, :] = item
    turned = stack_ref[...].T

    def column(index, c):
        return turned[:, index * chunks + c:index * chunks + c + 1]

    for q in range(chunks // per_query):
        mine = range(q * per_query, (q + 1) * per_query)
        ideal = jnp.zeros((1, 1), F32)
        sums = []
        for j in mine:
            srow, grow, drow, krow = score[j:j + 1], gain[j:j + 1], disc[j:j + 1], key[j:j + 1]
            place = jnp.zeros((1, LANES), F32)
            push = jnp.zeros((1, LANES), F32)
            curve = jnp.zeros((1, LANES), F32)
            for i in mine:
                place += jnp.sum(jnp.where(column(3, i) > krow, 1.0, 0.0), axis=0, keepdims=True)
                apart = column(0, i) - srow
                step = column(1, i) - grow
                chance = 1.0 / (1.0 + jnp.exp(jnp.where(step > 0.0, apart, -apart)))
                part = chance * jnp.abs(column(2, i) - drow) * column(4, i)
                signed = part * step
                push += jnp.sum(signed, axis=0, keepdims=True)
                curve += jnp.sum(jnp.abs(signed) * (1.0 - chance), axis=0, keepdims=True)
            top = livef[j:j + 1] * grow * (math.log(2.0) / jnp.log(place + 2.0))
            ideal += jnp.sum(top, axis=1, keepdims=True)
            sums.append((push, curve))
        scaling = 1.0 / jnp.maximum(ideal, 1.0)
        for j, (push, curve) in zip(mine, sums):
            grad_ref[j:j + 1, :] = push * livef[j:j + 1] * scaling
            hess_ref[j:j + 1, :] = curve * livef[j:j + 1] * scaling

    sub = lax.broadcasted_iota(jnp.int32, (leaves, LANES), 0)
    own = [leaf_ref[c:c + 1, :] == sub for c in range(chunks)]
    grad, hess, leaf = grad_ref[...], hess_ref[...], leaf_ref[...].astype(F32)
    for i in range(n):
        base = turns * chunks
        for turn in range(turns):
            e = slot_of(i, turn, n)
            if e < picked:
                for c in range(chunks):
                    block = all_ref[e * leaves:(e + 1) * leaves, c * LANES:(c + 1) * LANES]
                    send_ref[i, turn * chunks + c:turn * chunks + c + 1, :] = jnp.sum(
                        jnp.where(own[c], block, 0.0), axis=0, keepdims=True)
            else:
                send_ref[i, turn * chunks:(turn + 1) * chunks, :] = jnp.zeros((chunks, LANES), F32)
        send_ref[i, base:base + chunks, :] = grad
        send_ref[i, base + chunks:base + 2 * chunks, :] = hess
        send_ref[i, base + 2 * chunks:base + 3 * chunks, :] = leaf
        rest = send_ref.shape[1] - base - 3 * chunks
        if rest:
            send_ref[i, base + 3 * chunks:, :] = jnp.zeros((rest, LANES), F32)


def shared_kernel(n, turns, chunks, picked, votes_each, packed_ref, send_ref, count_ref, out_ref,
                  votes_ref, docs_ref, weight_ref, vs, vr, ds, dr, rs, rr, ls, lr, ss, sr):
    leaves, features = count_ref.shape
    chips = n // 2
    me = lax.axis_index("rows")
    core, chip = lax.rem(me, 2), me // 2

    def place_of(c):
        return jnp.where(c % 2 == 0, c // 2, chips - 1 - c // 2)

    def chip_at(p):
        return jnp.where(p < chips // 2, 2 * p, 2 * (chips - 1 - p) + 1)

    place = place_of(chip)

    def at(offset):
        return chip_at(lax.rem(place + offset + chips, chips)) * 2 + core

    sibling = me + 1 - 2 * core

    barrier = pltpu.get_barrier_semaphore()

    def greet(k, _):
        pl.semaphore_signal(barrier, inc=1, device_id={"rows": lax.rem(me + k, n)},
                            device_id_type=pl.DeviceIdType.MESH)
        return 0

    lax.fori_loop(1, n, greet, 0)
    pl.semaphore_wait(barrier, n - 1)

    def votes_copy(k):
        return pltpu.make_async_remote_copy(
            src_ref=packed_ref, dst_ref=votes_ref.at[me], send_sem=vs.at[k], recv_sem=vr.at[k],
            device_id={"rows": lax.rem(me + k, n)}, device_id_type=pl.DeviceIdType.MESH)

    def docs_copy(k):
        there = lax.rem(me + k, n)
        return pltpu.make_async_remote_copy(
            src_ref=send_ref.at[there], dst_ref=docs_ref.at[me], send_sem=ds.at[k],
            recv_sem=dr.at[k], device_id={"rows": there}, device_id_type=pl.DeviceIdType.MESH)

    def start_both(k, _):
        votes_copy(k).start()
        return 0

    def start_docs(k, _):
        docs_copy(k).start()
        return 0

    lax.fori_loop(1, n, start_both, 0)
    lax.fori_loop(1, n, start_docs, 0)
    votes_ref[me] = packed_ref[...]
    docs_ref[me] = send_ref[me]

    def wait_votes(k, _):
        votes_copy(k).wait()
        return 0

    lax.fori_loop(1, n, wait_votes, 0)
    groups = leaves // 8
    pitch = LANES // groups
    numbers = lax.broadcasted_iota(jnp.int32, (8, features), 1)

    def count(p, totals):
        tile = votes_ref[p]
        grown = []
        for g in range(groups):
            total = totals[g]
            for k in range(votes_each):
                total += jnp.where(tile[:, g * pitch + k:g * pitch + k + 1] == numbers, 1, 0)
            grown.append(total)
        return tuple(grown)

    totals = lax.fori_loop(0, n, count, (jnp.zeros((8, features), jnp.int32),) * groups)
    for g in range(groups):
        count_ref[g * 8:(g + 1) * 8, :] = totals[g]

    def wait_docs(k, _):
        docs_copy(k).wait()
        return 0

    lax.fori_loop(1, n, wait_docs, 0)
    sub = lax.broadcasted_iota(jnp.int32, (leaves, LANES), 0).astype(F32)
    base = turns * chunks

    def weigh(p, _):
        for c in range(chunks):
            own = docs_ref[p, base + 2 * chunks + c:base + 2 * chunks + c + 1, :] == sub
            for which in range(2):
                at_row = base + which * chunks + c
                left = docs_ref[p, at_row:at_row + 1, :]
                for term in range(TERMS):
                    piece = left.astype(BF16).astype(F32)
                    left = left - piece
                    at_weight = (term * 2 + which) * leaves
                    weight_ref[p, at_weight:at_weight + leaves, c * LANES:(c + 1) * LANES] = (
                        jnp.where(own, piece, 0.0).astype(BF16))
        return 0

    lax.fori_loop(0, n, weigh, 0)
    steps = lax.broadcasted_iota(jnp.int32, (B, LANES), 0).astype(F32)

    def tile_copy(slot, sems, rsems, index, there):
        return pltpu.make_async_remote_copy(
            src_ref=out_ref.at[slot], dst_ref=out_ref.at[slot], send_sem=sems.at[index],
            recv_sem=rsems.at[index], device_id={"rows": there},
            device_id_type=pl.DeviceIdType.MESH)

    far = chips // 2
    near = chips - 1 - far

    def right_copy(hop, turn):
        return tile_copy(slot_of(at(-hop), turn, n), rs, rr, hop * turns + turn, at(1))

    def left_copy(hop, turn):
        return tile_copy(slot_of(at(hop), turn, n), ls, lr, hop * turns + turn, at(-1))

    def sibling_copy(offset, turn):
        index = (offset + chips) % chips * turns + turn
        return tile_copy(slot_of(at(offset), turn, n), ss, sr, index, sibling)

    def exists(offset, turn):
        return slot_of(at(offset), turn, n) < picked

    def reach(hop, last_core):
        if hop <= near:
            return True
        if hop > far:
            return False
        return core == last_core

    def when(ok, also=True):
        if also is True:
            return pl.when(ok)
        return pl.when(jnp.logical_and(ok, also))

    for turn in range(turns):
        mine = slot_of(me, turn, n)

        @pl.when(mine < picked)
        def _(turn=turn, mine=mine):
            def add(p, total):
                tall = []
                for c in range(chunks):
                    bins = docs_ref[p, turn * chunks + c:turn * chunks + c + 1, :]
                    tall.append(jnp.where(bins <= steps, 1.0, 0.0).astype(BF16))
                return total + lax.dot_general(
                    weight_ref[p], jnp.concatenate(tall, axis=1), NT, preferred_element_type=F32)

            total = lax.fori_loop(0, n, add, jnp.zeros((TERMS * 2 * leaves, B), F32))
            both = total[:2 * leaves]
            for term in range(1, TERMS):
                both += total[term * 2 * leaves:(term + 1) * 2 * leaves]
            pg, ph = both[:leaves], both[leaves:]
            wg, wh = pg[:, B - 1:], ph[:, B - 1:]
            og, oh = wg - pg, wh - ph
            out_ref[mine] = (pg * pg / (ph + ridge_weight) + og * og / (oh + ridge_weight)
                             - wg * wg / (wh + ridge_weight))

        @pl.when(mine < picked)
        def _(turn=turn):
            right_copy(0, turn).start()
            left_copy(0, turn).start()
            sibling_copy(0, turn).start()

    for hop in range(1, far + 1):
        for turn in range(turns):
            arrives = reach(hop, 0)
            if arrives is not False:

                @when(exists(-hop, turn), arrives)
                def _(hop=hop, turn=turn):
                    tile_copy(slot_of(at(-hop), turn, n), rs, rr, (hop - 1) * turns + turn,
                              at(1)).wait_recv()
                    sibling_copy(-hop, turn).start()

                onward = reach(hop + 1, 0)
                if onward is not False:

                    @when(exists(-hop, turn), onward)
                    def _(hop=hop, turn=turn):
                        right_copy(hop, turn).start()

            arrives = reach(hop, 1)
            if arrives is not False:

                @when(exists(hop, turn), arrives)
                def _(hop=hop, turn=turn):
                    tile_copy(slot_of(at(hop), turn, n), ls, lr, (hop - 1) * turns + turn,
                              at(-1)).wait_recv()
                    sibling_copy(hop, turn).start()

                onward = reach(hop + 1, 1)
                if onward is not False:

                    @when(exists(hop, turn), onward)
                    def _(hop=hop, turn=turn):
                        left_copy(hop, turn).start()

    def other(offset, turn):
        return slot_of(at(offset) + 1 - 2 * core, turn, n)

    for turn in range(turns):
        for offset in range(chips):

            @pl.when(other(offset, turn) < picked)
            def _(offset=offset, turn=turn):
                tile_copy(other(offset, turn), ss, sr, offset * turns + turn, sibling).wait_recv()

            @pl.when(exists(offset, turn))
            def _(offset=offset, turn=turn):
                sibling_copy(offset, turn).wait_send()

        for hop in range(far):
            onward = reach(hop + 1, 0)
            if onward is not False:

                @when(exists(-hop, turn), onward)
                def _(hop=hop, turn=turn):
                    right_copy(hop, turn).wait_send()

            onward = reach(hop + 1, 1)
            if onward is not False:

                @when(exists(hop, turn), onward)
                def _(hop=hop, turn=turn):
                    left_copy(hop, turn).wait_send()


def on_device(n, feature_bin, doc_leaf, current_score, relevance, doc_rank, query_length,
              feature_votes, elected):
    docs, features = feature_bin.shape
    leaves, picked = elected.shape
    each = feature_votes.shape[2]
    turns = -(-picked // n)
    chunks = docs // LANES
    rows = -(-(turns + 3) * chunks // 8) * 8
    chips = n // 2
    far = chips // 2

    def lay(a):
        return a.reshape(chunks, LANES)

    send, gradient, hessian, packed = pl.pallas_call(
        functools.partial(local_kernel, n, turns),
        out_shape=(
            jax.ShapeDtypeStruct((n, rows, LANES), F32),
            jax.ShapeDtypeStruct((chunks, LANES), F32),
            jax.ShapeDtypeStruct((chunks, LANES), F32),
            jax.ShapeDtypeStruct((8, LANES), jnp.int32),
        ),
        in_specs=[VMEM] * 5 + [pl.BlockSpec(memory_space=pltpu.SMEM)] + [VMEM] * 2,
        out_specs=(VMEM,) * 4,
        scratch_shapes=[
            pltpu.VMEM((picked * leaves, features), BF16),
            pltpu.VMEM((LANES, LANES), F32),
            pltpu.VMEM((picked * leaves, docs), F32),
        ],
        compiler_params=pltpu.CompilerParams(vmem_limit_bytes=40 * 2**20),
        name="local",
    )(feature_bin, lay(doc_leaf), lay(current_score), lay(relevance), lay(doc_rank), query_length,
      elected, feature_votes)

    dma = pltpu.SemaphoreType.DMA
    vote_count, gathered = pl.pallas_call(
        functools.partial(shared_kernel, n, turns, chunks, picked, each),
        out_shape=(
            jax.ShapeDtypeStruct((leaves, features), jnp.int32),
            jax.ShapeDtypeStruct((picked, leaves, B), F32),
        ),
        in_specs=[VMEM] * 2,
        out_specs=(VMEM,) * 2,
        scratch_shapes=[
            pltpu.VMEM((n, 8, LANES), jnp.int32),
            pltpu.VMEM((n, rows, LANES), F32),
            pltpu.VMEM((n, TERMS * 2 * leaves, docs), BF16),
            dma((n,)), dma((n,)), dma((n,)), dma((n,)),
            dma((far * turns,)), dma((far * turns,)),
            dma((far * turns,)), dma((far * turns,)),
            dma((chips * turns,)), dma((chips * turns,)),
        ],
        compiler_params=pltpu.CompilerParams(
            collective_id=0, has_side_effects=True, vmem_limit_bytes=48 * 2**20),
        name="shared",
    )(packed, send)
    split_gain = jnp.transpose(gathered, (1, 0, 2))
    return gradient.reshape(-1), hessian.reshape(-1), vote_count, split_gain


def solution(mesh):
    n = mesh.shape["rows"]
    return jax.shard_map(
        functools.partial(on_device, n),
        mesh=mesh,
        in_specs=(
            P(("parts", "rows"), None),
            P(("parts", "rows")),
            P(("parts", "rows")),
            P(("parts", "rows")),
            P(("parts", "rows")),
            P(("parts", "rows")),
            P(("parts", "rows"), None, None),
            P("parts", None),
        ),
        out_specs=(
            P(("parts", "rows")),
            P(("parts", "rows")),
            P("parts", None),
            P("parts", None, None),
        ),
        check_vma=False,
    )
```

time: 417 us -> 51 us (0.12); the launches traced: 409 us -> 50.7 us
  local copies, waits for them, and re-layouts: 189 us -> 5.14 us
  other arithmetic: 92.9 us -> 0 us
  waiting for transfers between devices: 74.4 us -> 0 us
  Pallas kernels: 0 us -> 44.9 us
  blocking collectives: 24.5 us -> 0 us
  between operations: 14.3 us -> 0.72 us
  matrix products: 12 us -> 0 us
    gather x5 -> x0, local copies, waits for them, and re-layouts: 164 us -> none  [build_histogram(): chosen = jnp.take_along_axis(feature_bin, columns, axis=1)]
    psum x1 -> x0, waiting for transfers between devices: 74.4 us -> none  [on_device(): summed = lax.psum(histogram, 'rows')]
    another operation x5 -> x0, other arithmetic: 72.3 us -> none
    pallas_call x0 -> x2, Pallas kernels: none -> 44.9 us  [the longest x1 42.6 us: on_device(): pl.pallas_call(functools.partial(shared_kernel, n, turns, chunks, picked,...]
    all_gather x1 -> x0, blocking collectives: 24.5 us -> none  [on_device(): all_votes = lax.all_gather(feature_votes, 'rows', axis=0, tiled=True)]
    dot_general x2 -> x0, matrix products: 12 us -> none  [the longest x1 11 us: add_block(): return total + jnp.dot(weighted.T, onehot, precision=lax.Precision.HIGHEST)]
    another operation x4 -> x0, local copies, waits for them, and re-layouts: 9.1 us -> none
    sub x8 -> x0, other arithmetic: 7.9 us -> none  [the longest x1 3.07 us: split_score(): prefix[0] * prefix[0] / (prefix[1] + ridge_weight)]
  transfers between devices with their start and end apart: 1 -> 0, of which waited for: 1 -> 0; matrix products, arithmetic and copies ran while one was open for 1% -> 0% of each run, Pallas kernels for 0% -> 0%
where the time goes in v1:
time: 51 us; the launch traced here: 50.7 us
  Pallas kernels  44.9 us (88%)
  local copies, waits for them, and re-layouts  5.14 us (10%)
  between operations  0.72 us (1%)
    pallas_call x1, Pallas kernels, on_device(): pl.pallas_call(functools.partial(shared_kernel, n, turns, chunks, picked,...  42.6 us
    unnamed x16, local copies, waits for them, and re-layouts  5.14 us
    pallas_call x1, Pallas kernels, on_device(): pl.pallas_call(functools.partial(local_kernel, n, turns), out_shape=(jax....  2.26 us

profile of v1, /device:TPU:0, one launch (start us, length us, event | category | flops | bytes accessed | tf_op | source)
XLA Modules:
  0.0 50.7 jit_solution(11254974136467880067)
XLA Ops:
  0.6 0.8 %copy.13.votes_ref = s32[1,32,20]{2,1,0:T(8,128)S(1)} copy(s32[1,32,20]{1,0,2:T(1,128)} %param.14) | data formatting | bytes 5120 | tf_op args[6]
  1.4 0.0 copy-start
  1.4 0.0 copy-start.1
  1.4 0.0 copy-start.2
  1.4 0.0 copy-start.3
  1.4 0.0 copy-start.4
  1.4 0.0 copy-start.5
  1.5 1.9 %copy.12.fb_ref = s32[512,700]{1,0:T(8,128)S(1)} copy(s32[512,700]{0,1:T(8,128)} %param.8) | data formatting | bytes 2867200 | tf_op args[0]
  3.3 0.0 copy-done
  3.3 0.0 copy-done.1
  3.4 0.0 copy-done.2
  3.4 0.0 copy-done.3
  3.4 0.0 copy-done.4
  3.4 0.0 copy-done.5
  3.4 2.3 %local.1 = (f32[16,24,128]{2,1,0:T(8,128)S(1)}, f32[4,128]{1,0:T(4,128)}, f32[4,128]{1,0:T(4,128)}, s32[8,128]{1,0:T(8,128)S(1)}) custom-call(s32[512,700]{1,0:T(8,128)S(1)} %copy.12.fb_ref, s32[4,128]{1,0:T(4,128)S(1)} %bitcast.8, f32[4,128]{1,0:T(4,128)S(1)} %bitcast.9, s32[4,128]{1,0:T(4,128)S(1)} %bitcast.10, s32[4,128]{1,0:T(4,128)S(1)} %bitcast.11, ...), custom_call_target="tpu_custom_call" | custom-call | tf_op jit(solution)/shard_map/local/pallas_call | solution.py:358
  5.7 42.6 %shared.1 = (s32[32,700]{1,0:T(8,128)S(1)}, f32[40,32,256]{2,1,0:T(8,128)S(1)}) custom-call(s32[8,128]{1,0:T(8,128)S(1)} %get-tuple-element.12.packed_ref, f32[16,24,128]{2,1,0:T(8,128)S(1)} %get-tuple-element.13.send_ref), custom_call_target="tpu_custom_call" | custom-call | tf_op jit(solution)/shard_map/shared/pallas_call | solution.py:379
  48.3 1.8 %copy.14 = f32[32,40,256]{2,1,0:T(8,128)} copy(f32[32,40,256]{2,0,1:T(8,128)S(1)} %bitcast.7) | data formatting | bytes 2621440
  50.1 0.6 %copy.16 = s32[32,700]{1,0:T(8,128)} copy(s32[32,700]{1,0:T(8,128)S(1)} %get-tuple-element.26) | data formatting | bytes 179200
Async XLA Ops:
  1.4 1.9 %copy-start = (s32[32,40]{1,0:T(8,128)S(1)}, s32[32,40]{1,0:T(8,128)}, u32[]{:S(2)}) copy-start(s32[32,40]{1,0:T(8,128)} %elected_ref.1) | copy-start | bytes 15364
  1.4 1.9 %copy-start.1 = (s32[512]{0:T(512)S(1)}, s32[512]{0:T(512)}, u32[]{:S(2)}) copy-start(s32[512]{0:T(512)} %param.9) | copy-start | bytes 6148
  1.4 1.9 %copy-start.2 = (f32[512]{0:T(512)S(1)}, f32[512]{0:T(512)}, u32[]{:S(2)}) copy-start(f32[512]{0:T(512)} %param.10) | copy-start | bytes 6148
  1.4 2.0 %copy-start.3 = (s32[512]{0:T(512)S(1)}, s32[512]{0:T(512)}, u32[]{:S(2)}) copy-start(s32[512]{0:T(512)} %param.11) | copy-start | bytes 6148
  1.4 1.9 %copy-start.4 = (s32[512]{0:T(512)S(1)}, s32[512]{0:T(512)}, u32[]{:S(2)}) copy-start(s32[512]{0:T(512)} %param.12) | copy-start | bytes 6148
  1.4 1.9 %copy-start.5 = (s32[2]{0:T(128)S(1)}, s32[2]{0:T(128)}, u32[]{:S(2)}) copy-start(s32[2]{0:T(128)} %qlen_ref.1) | copy-start | bytes 28

commit v2 on v1

v2 whole, which is shorter than its diff:
```python
import functools
import math

import jax
import jax.numpy as jnp
from jax import lax
from jax.experimental import pallas as pl
from jax.experimental.pallas import tpu as pltpu
from jax.sharding import PartitionSpec as P

B = 256
QMAX = 256
LANES = 128
SUB = 16
TERMS = 2
UNROLL = 4

ridge_weight = 1.0
F32 = jnp.float32
BF16 = jnp.bfloat16
NT = (((1,), (1,)), ((), ()))
NN = (((1,), (0,)), ((), ()))
VMEM = pl.BlockSpec(memory_space=pltpu.VMEM)
MESH = pl.DeviceIdType.MESH


def slot_of(owner, turn, n):
    return turn * n + (owner % 2) * (n // 2) + owner // 2


def pair_terms(chunks, leaf_ref, score_ref, rel_ref, rank_ref, qlen_ref, votes_ref, packed_ref,
               stack_ref, grad_ref, hess_ref, leaves):
    per_query = QMAX // LANES
    each = votes_ref.shape[0]
    rel = rel_ref[...].astype(F32)
    gain = jnp.exp2(rel) - 1.0
    disc = math.log(2.0) / jnp.log(rank_ref[...].astype(F32) + 2.0)
    row = lax.broadcasted_iota(jnp.int32, (chunks, LANES), 0)
    slot = (row % per_query) * LANES + lax.broadcasted_iota(jnp.int32, (chunks, LANES), 1)
    length = jnp.zeros((chunks, LANES), jnp.int32)
    for q in range(chunks // per_query):
        length = jnp.where(row // per_query == q, qlen_ref[q], length)
    live = slot < length
    livef = jnp.where(live, 1.0, 0.0)
    key = rel * float(QMAX) + (QMAX - 1 - slot).astype(F32)
    score = score_ref[...]
    stack_ref[...] = jnp.zeros(stack_ref.shape, F32)
    items = (score, gain, disc, jnp.where(live, key, -1.0), livef)
    for index, item in enumerate(items):
        stack_ref[index * chunks:(index + 1) * chunks, :] = item
    first = len(items) * chunks
    for k in range(each):
        stack_ref[first + k:first + k + 1, 0:leaves] = votes_ref[k].astype(F32)
    turned = stack_ref[...].T

    groups = leaves // 8
    pitch = LANES // groups
    packed_ref[...] = jnp.full(packed_ref.shape, -1, jnp.int32)
    for g in range(groups):
        packed_ref[:, g * pitch:g * pitch + each] = turned[
            g * 8:(g + 1) * 8, first:first + each].astype(jnp.int32)

    def column(index, c):
        return turned[:, index * chunks + c:index * chunks + c + 1]

    for q in range(chunks // per_query):
        mine = range(q * per_query, (q + 1) * per_query)
        ideal = jnp.zeros((1, 1), F32)
        sums = []
        for j in mine:
            srow, grow, drow, krow = score[j:j + 1], gain[j:j + 1], disc[j:j + 1], key[j:j + 1]
            place = jnp.zeros((1, LANES), F32)
            push = jnp.zeros((1, LANES), F32)
            curve = jnp.zeros((1, LANES), F32)
            for i in mine:
                place += jnp.sum(jnp.where(column(3, i) > krow, 1.0, 0.0), axis=0, keepdims=True)
                apart = column(0, i) - srow
                step = column(1, i) - grow
                chance = 1.0 / (1.0 + jnp.exp(jnp.where(step > 0.0, apart, -apart)))
                part = chance * jnp.abs(column(2, i) - drow) * column(4, i)
                signed = part * step
                push += jnp.sum(signed, axis=0, keepdims=True)
                curve += jnp.sum(jnp.abs(signed) * (1.0 - chance), axis=0, keepdims=True)
            top = livef[j:j + 1] * grow * (math.log(2.0) / jnp.log(place + 2.0))
            ideal += jnp.sum(top, axis=1, keepdims=True)
            sums.append((push, curve))
        scaling = 1.0 / jnp.maximum(ideal, 1.0)
        for j, (push, curve) in zip(mine, sums):
            grad_ref[j:j + 1, :] = push * livef[j:j + 1] * scaling
            hess_ref[j:j + 1, :] = curve * livef[j:j + 1] * scaling


def kernel(n, turns, fb_hbm, leaf_hbm, score_hbm, rel_hbm, rank_hbm, qlen_hbm, elected_hbm,
           votes_hbm, grad_ref, hess_ref, count_ref, gain_hbm,
           fb_ref, leaf_ref, score_ref, rel_ref, rank_ref, qlen_ref, elected_ref, votes_in,
           hot_ref, stack_ref, all_ref, packed_ref, send_ref,
           votes_ref, docs_ref, weight_ref, out_ref, load_sem, save_sem, vs, vr, ds, dr, zs, zr, ys, yr, ss, sr):
    features, docs = fb_ref.shape
    leaves, picked = elected_ref.shape
    votes_each = votes_in.shape[0]
    chunks = docs // LANES
    base = turns * chunks
    chips = n // 2
    lines = chips // 2
    me = lax.axis_index("rows")
    core, side, line = me % 2, (me // 2) % 2, me // 4

    def device(line_, side_, core_):
        return line_ * 4 + side_ * 2 + core_

    barrier = pltpu.get_barrier_semaphore()

    def greet(k, _):
        pl.semaphore_signal(barrier, inc=1, device_id={"rows": lax.rem(me + k, n)},
                            device_id_type=MESH)
        return 0

    lax.fori_loop(1, n, greet, 0)
    loads = [
        pltpu.make_async_copy(there, here, load_sem.at[index])
        for index, (there, here) in enumerate((
            (leaf_hbm, leaf_ref), (score_hbm, score_ref), (rel_hbm, rel_ref),
            (rank_hbm, rank_ref), (qlen_hbm, qlen_ref), (votes_hbm, votes_in),
            (elected_hbm, elected_ref), (fb_hbm, fb_ref)))
    ]
    for load in loads:
        load.start()
    for load in loads[:-1]:
        load.wait()

    pair_terms(chunks, leaf_ref, score_ref, rel_ref, rank_ref, qlen_ref, votes_in, packed_ref,
               stack_ref, grad_ref, hess_ref, leaves)

    lanes = lax.broadcasted_iota(jnp.int32, (leaves, features), 1)
    for e in range(picked):
        hot_ref[e * leaves:(e + 1) * leaves, :] = jnp.where(
            elected_ref[:, e:e + 1] == lanes, 1.0, 0.0).astype(BF16)
    loads[-1].wait()
    bins = fb_ref[...].astype(F32).astype(BF16)
    all_ref[...] = lax.dot_general(hot_ref[...], bins, NN, preferred_element_type=F32)

    sub = lax.broadcasted_iota(jnp.int32, (leaves, LANES), 0)
    own = [leaf_ref[c:c + 1, :] == sub for c in range(chunks)]
    grad, hess, leaf = grad_ref[...], hess_ref[...], leaf_ref[...].astype(F32)
    for i in range(n):
        for turn in range(turns):
            e = slot_of(i, turn, n)
            if e < picked:
                for c in range(chunks):
                    block = all_ref[e * leaves:(e + 1) * leaves, c * LANES:(c + 1) * LANES]
                    send_ref[i, turn * chunks + c:turn * chunks + c + 1, :] = jnp.sum(
                        jnp.where(own[c], block, 0.0), axis=0, keepdims=True)
            else:
                send_ref[i, turn * chunks:(turn + 1) * chunks, :] = jnp.zeros((chunks, LANES), F32)
        send_ref[i, base:base + chunks, :] = grad
        send_ref[i, base + chunks:base + 2 * chunks, :] = hess
        send_ref[i, base + 2 * chunks:base + 3 * chunks, :] = leaf
        rest = send_ref.shape[1] - base - 3 * chunks
        if rest:
            send_ref[i, base + 3 * chunks:, :] = jnp.zeros((rest, LANES), F32)

    pl.semaphore_wait(barrier, n - 1)

    def votes_copy(k):
        return pltpu.make_async_remote_copy(
            src_ref=packed_ref, dst_ref=votes_ref.at[me], send_sem=vs.at[k], recv_sem=vr.at[k],
            device_id={"rows": lax.rem(me + k, n)}, device_id_type=MESH)

    def docs_copy(k):
        there = lax.rem(me + k, n)
        return pltpu.make_async_remote_copy(
            src_ref=send_ref.at[there], dst_ref=docs_ref.at[me], send_sem=ds.at[k],
            recv_sem=dr.at[k], device_id={"rows": there}, device_id_type=MESH)

    def start_votes(k, _):
        votes_copy(k).start()
        return 0

    def start_docs(k, _):
        docs_copy(k).start()
        return 0

    lax.fori_loop(1, n, start_docs, 0)
    lax.fori_loop(1, n, start_votes, 0)
    votes_ref[me] = packed_ref[...]
    docs_ref[me] = send_ref[me]

    def wait_docs(k, _):
        docs_copy(k).wait()
        return 0

    lax.fori_loop(1, n, wait_docs, 0)
    subf = sub.astype(F32)

    def weigh(p, _):
        for c in range(chunks):
            own = docs_ref[p, base + 2 * chunks + c:base + 2 * chunks + c + 1, :] == subf
            for which in range(2):
                at_row = base + which * chunks + c
                left = docs_ref[p, at_row:at_row + 1, :]
                for term in range(TERMS):
                    piece = left.astype(BF16).astype(F32)
                    left = left - piece
                    at_weight = (term * 2 + which) * leaves
                    weight_ref[p, at_weight:at_weight + leaves, c * LANES:(c + 1) * LANES] = (
                        jnp.where(own, piece, 0.0).astype(BF16))
        return 0

    lax.fori_loop(0, n, weigh, 0)
    steps = [lax.broadcasted_iota(jnp.int32, (SUB, LANES), 0).astype(F32).astype(BF16)
             + jnp.asarray(first, BF16) for first in range(0, B, SUB)]
    one, zero = jnp.ones((SUB, LANES), BF16), jnp.zeros((SUB, LANES), BF16)

    def exists(owner, turn):
        return slot_of(owner, turn, n) < picked

    def tile_copy(slot, sems, rsems, index, there):
        return pltpu.make_async_remote_copy(
            src_ref=out_ref.at[slot], dst_ref=out_ref.at[slot], send_sem=sems.at[index],
            recv_sem=rsems.at[index], device_id={"rows": there}, device_id_type=MESH)

    def line_copy(k, turn):
        return tile_copy(slot_of(me, turn, n), zs, zr, k * turns + turn,
                         device(lax.rem(line + k, lines), side, core))

    def side_copy(line_, side_, turn):
        return tile_copy(slot_of(device(line_, side_, core), turn, n), ys, yr,
                         line_ * turns + turn, device(line, 1 - side, core))

    def core_copy(line_, side_, core_, turn):
        return tile_copy(slot_of(device(line_, side_, core_), turn, n), ss, sr,
                         (line_ * 2 + side_) * turns + turn, device(line, side, 1 - core))

    def save(owner, turn):
        slot = slot_of(owner, turn, n)
        return pltpu.make_async_copy(out_ref.at[slot], gain_hbm.at[slot], save_sem.at[slot])

    def guarded(owner, turn, action):
        @pl.when(exists(owner, turn))
        def _():
            action()

    for turn in range(turns):
        def work(turn=turn):
            def add(p, total):
                tall = []
                for c in range(chunks):
                    row = docs_ref[p, turn * chunks + c:turn * chunks + c + 1, :]
                    row = jnp.broadcast_to(row, (SUB, LANES)).astype(BF16)
                    tall.append(jnp.concatenate(
                        [jnp.where(row <= step, one, zero) for step in steps], axis=0))
                return total + lax.dot_general(
                    jnp.concatenate(tall, axis=1), weight_ref[p], NT, preferred_element_type=F32)

            total = lax.fori_loop(
                0, n, add, jnp.zeros((B, TERMS * 2 * leaves), F32), unroll=UNROLL).T
            both = total[:2 * leaves]
            for term in range(1, TERMS):
                both += total[term * 2 * leaves:(term + 1) * 2 * leaves]
            pg, ph = both[:leaves], both[leaves:]
            wg, wh = pg[:, B - 1:], ph[:, B - 1:]
            og, oh = wg - pg, wh - ph
            out_ref[slot_of(me, turn, n)] = (
                pg * pg / (ph + ridge_weight) + og * og / (oh + ridge_weight)
                - wg * wg / (wh + ridge_weight))

        def begin(turn=turn):
            side_copy(line, side, turn).start()
            for k in range(1, lines):
                line_copy(k, turn).start()
            core_copy(line, side, core, turn).start()
            save(me, turn).start()

        guarded(me, turn, work)
        guarded(me, turn, begin)

    def wait_votes(k, _):
        votes_copy(k).wait()
        return 0

    lax.fori_loop(1, n, wait_votes, 0)
    groups = leaves // 8
    pitch = LANES // groups
    numbers = lax.broadcasted_iota(jnp.int32, (8, features), 1)

    def count(p, totals):
        tile = votes_ref[p]
        grown = []
        for g in range(groups):
            total = totals[g]
            for k in range(votes_each):
                total += jnp.where(tile[:, g * pitch + k:g * pitch + k + 1] == numbers, 1, 0)
            grown.append(total)
        return tuple(grown)

    totals = lax.fori_loop(0, n, count, (jnp.zeros((8, features), jnp.int32),) * groups)
    for g in range(groups):
        count_ref[g * 8:(g + 1) * 8, :] = totals[g]

    for turn in range(turns):
        for k in range(1, lines):
            def pass_on(turn=turn, k=k):
                source = lax.rem(line + lines - k, lines)
                tile_copy(slot_of(device(source, side, core), turn, n), zs, zr, k * turns + turn,
                          device(lax.rem(line + k, lines), side, core)).wait_recv()
                side_copy(source, side, turn).start()
                core_copy(source, side, core, turn).start()
                save(device(source, side, core), turn).start()

            guarded(device(lax.rem(line + lines - k, lines), side, core), turn, pass_on)

    for turn in range(turns):
        for k in range(lines):
            def cross(turn=turn, k=k):
                source = lax.rem(line + lines - k, lines)
                side_copy(source, 1 - side, turn).wait_recv()
                core_copy(source, 1 - side, core, turn).start()
                save(device(source, 1 - side, core), turn).start()

            guarded(device(lax.rem(line + lines - k, lines), 1 - side, core), turn, cross)

    for turn in range(turns):
        for line_ in range(lines):
            for side_ in range(2):
                def last(turn=turn, line_=line_, side_=side_):
                    core_copy(line_, side_, 1 - core, turn).wait_recv()
                    save(device(line_, side_, 1 - core), turn).start()

                guarded(device(line_, side_, 1 - core), turn, last)
                guarded(device(line_, side_, core), turn,
                        lambda: core_copy(line_, side_, core, turn).wait_send())
            guarded(device(line_, side, core), turn,
                    lambda: side_copy(line_, side, turn).wait_send())
        for k in range(1, lines):
            guarded(me, turn, lambda: line_copy(k, turn).wait_send())
        for owner in range(n):
            if slot_of(owner, turn, n) < picked:
                save(owner, turn).wait()


def finish(grad_in, hess_in, count_in, gathered, grad_ref, hess_ref, count_ref, out_ref):
    grad_ref[...] = grad_in[...]
    hess_ref[...] = hess_in[...]
    count_ref[...] = count_in[...]
    out_ref[...] = jnp.swapaxes(gathered[...], 0, 1)


def on_device(n, feature_bin, doc_leaf, current_score, relevance, doc_rank, query_length,
              feature_votes, elected):
    docs, features = feature_bin.shape
    leaves, picked = elected.shape
    each = feature_votes.shape[2]
    turns = -(-picked // n)
    chunks = docs // LANES
    rows = -(-(turns + 3) * chunks // 8) * 8
    chips = n // 2
    lines = chips // 2

    def lay(a):
        return a.reshape(chunks, LANES)

    dma = pltpu.SemaphoreType.DMA
    gradient, hessian, vote_count, gathered = pl.pallas_call(
        functools.partial(kernel, n, turns),
        out_shape=(
            jax.ShapeDtypeStruct((chunks, LANES), F32),
            jax.ShapeDtypeStruct((chunks, LANES), F32),
            jax.ShapeDtypeStruct((leaves, features), jnp.int32),
            jax.ShapeDtypeStruct((picked, leaves, B), F32),
        ),
        in_specs=[pl.BlockSpec(memory_space=pltpu.HBM)] * 8,
        out_specs=(VMEM,) * 3 + (pl.BlockSpec(memory_space=pltpu.HBM),),
        scratch_shapes=[
            pltpu.VMEM((features, docs), jnp.int32),
            pltpu.VMEM((chunks, LANES), jnp.int32),
            pltpu.VMEM((chunks, LANES), F32),
            pltpu.VMEM((chunks, LANES), jnp.int32),
            pltpu.VMEM((chunks, LANES), jnp.int32),
            pltpu.SMEM(query_length.shape, jnp.int32),
            pltpu.VMEM((leaves, picked), jnp.int32),
            pltpu.VMEM((each, 1, leaves), jnp.int32),
            pltpu.VMEM((picked * leaves, features), BF16),
            pltpu.VMEM((LANES, LANES), F32),
            pltpu.VMEM((picked * leaves, docs), F32),
            pltpu.VMEM((8, LANES), jnp.int32),
            pltpu.VMEM((n, rows, LANES), F32),
            pltpu.VMEM((n, 8, LANES), jnp.int32),
            pltpu.VMEM((n, rows, LANES), F32),
            pltpu.VMEM((n, TERMS * 2 * leaves, docs), BF16),
            pltpu.VMEM((picked, leaves, B), F32),
            dma((8,)),
            dma((picked,)),
            dma((n,)), dma((n,)), dma((n,)), dma((n,)),
            dma((lines * turns,)), dma((lines * turns,)),
            dma((lines * turns,)), dma((lines * turns,)),
            dma((chips * turns,)), dma((chips * turns,)),
        ],
        compiler_params=pltpu.CompilerParams(
            collective_id=0, has_side_effects=True, vmem_limit_bytes=63 * 2**20),
        name="round",
    )(feature_bin.T, lay(doc_leaf), lay(current_score), lay(relevance), lay(doc_rank),
      query_length, elected, jnp.transpose(feature_votes, (2, 0, 1)))
    step = 8
    gradient, hessian, vote_count, split_gain = pl.pallas_call(
        finish,
        grid=(leaves // step,),
        out_shape=(
            jax.ShapeDtypeStruct((chunks, LANES), F32),
            jax.ShapeDtypeStruct((chunks, LANES), F32),
            jax.ShapeDtypeStruct((leaves, features), jnp.int32),
            jax.ShapeDtypeStruct((leaves, picked, B), F32),
        ),
        in_specs=[
            pl.BlockSpec((chunks, LANES), lambda i: (0, 0)),
            pl.BlockSpec((chunks, LANES), lambda i: (0, 0)),
            pl.BlockSpec((step, features), lambda i: (i, 0)),
            pl.BlockSpec((picked, step, B), lambda i: (0, i, 0)),
        ],
        out_specs=(
            pl.BlockSpec((chunks, LANES), lambda i: (0, 0)),
            pl.BlockSpec((chunks, LANES), lambda i: (0, 0)),
            pl.BlockSpec((step, features), lambda i: (i, 0)),
            pl.BlockSpec((step, picked, B), lambda i: (i, 0, 0)),
        ),
        compiler_params=pltpu.CompilerParams(vmem_limit_bytes=63 * 2**20),
        name="finish",
    )(gradient, hessian, vote_count, gathered)
    return gradient.reshape(-1), hessian.reshape(-1), vote_count, split_gain


def solution(mesh):
    n = mesh.shape["rows"]
    return jax.shard_map(
        functools.partial(on_device, n),
        mesh=mesh,
        in_specs=(
            P(("parts", "rows"), None),
            P(("parts", "rows")),
            P(("parts", "rows")),
            P(("parts", "rows")),
            P(("parts", "rows")),
            P(("parts", "rows")),
            P(("parts", "rows"), None, None),
            P("parts", None),
        ),
        out_specs=(
            P(("parts", "rows")),
            P(("parts", "rows")),
            P("parts", None),
            P("parts", None, None),
        ),
        check_vma=False,
    )
```

time: 51 us -> 38.8 us (0.76)
  Pallas kernels: 44.9 us -> 38 us
  local copies, waits for them, and re-layouts: 5.14 us -> 0 us
    pallas_call x2, Pallas kernels: 44.9 us -> 38 us  [the longest x1 34.3 us: on_device(): pl.pallas_call(functools.partial(kernel, n, turns), out_shape=(jax.ShapeD...]
    unnamed x16 -> x0, local copies, waits for them, and re-layouts: 5.14 us -> none
where the time goes in v2:
time: 38.8 us; the launch traced here: 38.6 us
  Pallas kernels  38 us (98%)
  between operations  0.64 us (2%)
    pallas_call x1, Pallas kernels, on_device(): pl.pallas_call(functools.partial(kernel, n, turns), out_shape=(jax.ShapeD...  34.3 us
    pallas_call x1, Pallas kernels, on_device(): pl.pallas_call(finish, grid=(leaves // step,), out_shape=(jax.ShapeDtypeS...  3.62 us

profile of v2, /device:TPU:0, one launch (start us, length us, event | category | flops | bytes accessed | tf_op | source)
XLA Modules:
  0.0 38.6 jit_solution(14714286717837428077)
XLA Ops:
  0.6 34.3 %round.1 = (f32[4,128]{1,0:T(4,128)}, f32[4,128]{1,0:T(4,128)}, s32[32,700]{1,0:T(8,128)}, f32[40,32,256]{2,1,0:T(8,128)}) custom-call(s32[700,512]{1,0:T(8,128)} %bitcast.8, s32[4,128]{1,0:T(4,128)} %bitcast.10, f32[4,128]{1,0:T(4,128)} %bitcast.11, s32[4,128]{1,0:T(4,128)} %bitcast.12, s32[4,128]{1,0:T(4,128)} %bitcast.13, s32[2]{0:T(128)} %qlen_hbm.1, ...), custom_call_target="tpu_custom_call" | custom-call | tf_op jit(solution)/shard_map/round/pallas_call | solution.py:363
  35.0 3.6 %finish.1 = (f32[4,128]{1,0:T(4,128)}, f32[4,128]{1,0:T(4,128)}, s32[32,700]{1,0:T(8,128)}, f32[32,40,256]{2,1,0:T(8,128)}) custom-call(f32[4,128]{1,0:T(4,128)} %get-tuple-element.12.grad_in, f32[4,128]{1,0:T(4,128)} %get-tuple-element.13.hess_in, s32[32,700]{1,0:T(8,128)} %get-tuple-element.14.count_in, f32[40,32,256]{2,1,0:T(8,128)} %get-tuple-element.15.gathered), custom_call_target="tpu_custom_call" | custom-call | tf_op jit(solution)/shard_map/finish/pallas_call | solution.py:404

commit v3 on v2

--- a/solution.py
+++ b/solution.py
@@ -13,7 +13,7 @@
 LANES = 128
 SUB = 16
 TERMS = 2
-UNROLL = 4
+UNROLL = 16
 
 ridge_weight = 1.0
 F32 = jnp.float32
@@ -181,7 +181,6 @@
         return 0
 
     lax.fori_loop(1, n, start_docs, 0)
-    lax.fori_loop(1, n, start_votes, 0)
     votes_ref[me] = packed_ref[...]
     docs_ref[me] = send_ref[me]
 
@@ -190,6 +189,7 @@
         return 0
 
     lax.fori_loop(1, n, wait_docs, 0)
+    lax.fori_loop(1, n, start_votes, 0)
     subf = sub.astype(F32)
 
     def weigh(p, _):
@@ -278,7 +278,6 @@
         votes_copy(k).wait()
         return 0
 
-    lax.fori_loop(1, n, wait_votes, 0)
     groups = leaves // 8
     pitch = LANES // groups
     numbers = lax.broadcasted_iota(jnp.int32, (8, features), 1)
@@ -293,11 +292,21 @@
             grown.append(total)
         return tuple(grown)
 
-    totals = lax.fori_loop(0, n, count, (jnp.zeros((8, features), jnp.int32),) * groups)
-    for g in range(groups):
-        count_ref[g * 8:(g + 1) * 8, :] = totals[g]
+    shares = turns + 1
+
+    def count_share(share):
+        low, high = share * n // shares, (share + 1) * n // shares
+        if share == 0:
+            lax.fori_loop(1, n, wait_votes, 0)
+            start = (jnp.zeros((8, features), jnp.int32),) * groups
+        else:
+            start = tuple(count_ref[g * 8:(g + 1) * 8, :] for g in range(groups))
+        totals = lax.fori_loop(low, high, count, start)
+        for g in range(groups):
+            count_ref[g * 8:(g + 1) * 8, :] = totals[g]
 
     for turn in range(turns):
+        count_share(turn)
         for k in range(1, lines):
             def pass_on(turn=turn, k=k):
                 source = lax.rem(line + lines - k, lines)
@@ -309,6 +318,7 @@
 
             guarded(device(lax.rem(line + lines - k, lines), side, core), turn, pass_on)
 
+    count_share(turns)
     for turn in range(turns):
         for k in range(lines):
             def cross(turn=turn, k=k):
@@ -400,7 +410,7 @@
         name="round",
     )(feature_bin.T, lay(doc_leaf), lay(current_score), lay(relevance), lay(doc_rank),
       query_length, elected, jnp.transpose(feature_votes, (2, 0, 1)))
-    step = 8
+    step = 16
     gradient, hessian, vote_count, split_gain = pl.pallas_call(
         finish,
         grid=(leaves // step,),

time: 38.8 us -> 34 us (0.88)
  Pallas kernels: 38 us -> 32.9 us
    pallas_call x1, Pallas kernels: 34.3 us -> 30.5 us  [on_device(): pl.pallas_call(functools.partial(kernel, n, turns), out_shape=(jax.ShapeD...]
    pallas_call x1, Pallas kernels: 3.62 us -> 2.36 us  [on_device(): pl.pallas_call(finish, grid=(leaves // step,), out_shape=(jax.ShapeDtypeS...]
where the time goes in v3:
time: 34 us; the launch traced here: 33.5 us
  Pallas kernels  32.9 us (97%)
  between operations  0.64 us (2%)
    pallas_call x1, Pallas kernels, on_device(): pl.pallas_call(functools.partial(kernel, n, turns), out_shape=(jax.ShapeD...  30.5 us
    pallas_call x1, Pallas kernels, on_device(): pl.pallas_call(finish, grid=(leaves // step,), out_shape=(jax.ShapeDtypeS...  2.36 us

profile of v3, /device:TPU:0, one launch (start us, length us, event | category | flops | bytes accessed | tf_op | source)
XLA Modules:
  0.0 33.5 jit_solution(14909493890924529841)
XLA Ops:
  0.6 30.5 %round.1 = (f32[4,128]{1,0:T(4,128)}, f32[4,128]{1,0:T(4,128)}, s32[32,700]{1,0:T(8,128)}, f32[40,32,256]{2,1,0:T(8,128)}) custom-call(s32[700,512]{1,0:T(8,128)} %bitcast.8, s32[4,128]{1,0:T(4,128)} %bitcast.10, f32[4,128]{1,0:T(4,128)} %bitcast.11, s32[4,128]{1,0:T(4,128)} %bitcast.12, s32[4,128]{1,0:T(4,128)} %bitcast.13, s32[2]{0:T(128)} %qlen_hbm.1, ...), custom_call_target="tpu_custom_call" | custom-call | tf_op jit(solution)/shard_map/round/pallas_call | solution.py:373
  31.2 2.4 %finish.1 = (f32[4,128]{1,0:T(4,128)}, f32[4,128]{1,0:T(4,128)}, s32[32,700]{1,0:T(8,128)}, f32[32,40,256]{2,1,0:T(8,128)}) custom-call(f32[4,128]{1,0:T(4,128)} %get-tuple-element.12.grad_in, f32[4,128]{1,0:T(4,128)} %get-tuple-element.13.hess_in, s32[32,700]{1,0:T(8,128)} %get-tuple-element.14.count_in, f32[40,32,256]{2,1,0:T(8,128)} %get-tuple-element.15.gathered), custom_call_target="tpu_custom_call" | custom-call | tf_op jit(solution)/shard_map/finish/pallas_call | solution.py:414
